TPU v7x, 32 devices: a whole 2x2x4 slice. The times are simulated.
32 devices in a mesh: bank: 8 (over z, y), zero: 4 (over x, core).
Axes of the slice: x: 2, y: 2, z: 4, core: 2. Of those that a mesh axis runs over, the one named last changes fastest.
Arguments:
- w_gate: float32 [64, 2048, 1024], P('bank', 'zero'), may hold values from -0.1875 to 0.1875
- avg_gate: float32 [64, 2048, 1024], P('bank', 'zero'), may hold values from -0.125 to 0.125
- w_up: float32 [64, 2048, 1024], P('bank', 'zero'), may hold values from -0.1875 to 0.1875
- avg_up: float32 [64, 2048, 1024], P('bank', 'zero'), may hold values from -0.125 to 0.125
- mix_share: float32 [64], P('bank'), may hold values from 0.2 to 0.8
- router_weight: float32 [2048, 64], P('zero', 'bank'), may hold values from -0.125 to 0.125
- router_gain: float32 [2048], P('zero'), may hold values from 0.25 to 1.75
Outputs:
- serve_gate: bfloat16 [64, 2048, 1024], P('bank')
- serve_up: bfloat16 [64, 2048, 1024], P('bank')
- scale_gate: float32 [64, 1024], P('bank')
- scale_up: float32 [64, 1024], P('bank')
- serve_router: bfloat16 [2048, 64], replicated
All inputs are finite; a program needn't handle non-finite values.
Results may differ from a plain program's by a relative error of at most 0.001.
Values may be sent and summed in bfloat16 or wider, within the bound.
A program may use at most 256 MiB of HBM per device.

v0:
```python
import jax
import jax.numpy as jnp
from jax import lax
from jax.sharding import PartitionSpec as P


def local(w_gate, avg_gate, w_up, avg_up, mix_share, router_weight, router_gain):
    fresh_gate = mix_share[:, None, None] * w_gate + (1.0 - mix_share[:, None, None]) * avg_gate
    fresh_up = mix_share[:, None, None] * w_up + (1.0 - mix_share[:, None, None]) * avg_up
    total_gate, total_up = lax.psum(
        (jnp.sum(fresh_gate * fresh_gate, axis=1), jnp.sum(fresh_up * fresh_up, axis=1)), "zero"
    )
    scale_gate = jnp.sqrt(total_gate)
    scale_up = jnp.sqrt(total_up)
    narrow_gate, narrow_up = (
        (fresh_gate / jnp.expand_dims(scale_gate, 1)).astype(jnp.bfloat16),
        (fresh_up / jnp.expand_dims(scale_up, 1)).astype(jnp.bfloat16),
    )
    serve_gate, serve_up = (
        lax.all_gather(narrow_gate, "zero", axis=1, tiled=True),
        lax.all_gather(narrow_up, "zero", axis=1, tiled=True),
    )
    part_router = (router_weight * router_gain[:, None]).astype(jnp.bfloat16)
    row_router = lax.all_gather(part_router, "zero", axis=0, tiled=True)
    serve_router = lax.all_gather(row_router, "bank", axis=1, tiled=True)
    return (serve_gate, serve_up, scale_gate, scale_up, serve_router)


def solution(mesh):
    placed = (
        P("bank", "zero", None),
        P("bank", "zero", None),
        P("bank", "zero", None),
        P("bank", "zero", None),
        P("bank"),
        P("zero", "bank"),
        P("zero"),
    )
    return jax.shard_map(
        local,
        mesh=mesh,
        in_specs=placed,
        out_specs=(
            P("bank", None, None),
            P("bank", None, None),
            P("bank", None),
            P("bank", None),
            P(),
        ),
        check_vma=False,
    )
```

profile of v0, /device:TPU:0, one launch (start us, length us, event | category | flops | bytes accessed | tf_op | source)
XLA Modules:
  0.0 555.7 jit_solution(15842915430037954129)
XLA Ops:
  7.2 0.0 all-reduce.3.cloned.1.call-start
  7.2 0.7 broadcast_subtract_fusion
  7.9 0.0 copy-start.3
  7.9 23.3 %multiply_reduce_fusion = (f32[8,1024]{1,0:T(8,128)}, f32[8,1024]{1,0:T(8,128)}) fusion(f32[8,512,1024]{2,1,0:T(8,128)} %param.10, f32[8]{0:T(128)S(1)} %broadcast_subtract_fusion, f32[8,512,1024]{2,1,0:T(8,128)} %param.9, f32[8]{0:T(128)} %param.11, f32[8,512,1024]{2,1,0:T(8,128)} %param.8, f32[8,512,1024]{2,1,0:T(8,128)} %param.7), kind=kLoop, calls=%fused_computation.1 | loop fusion | flops 41926656 | bytes 67174464 | tf_op jit(solution)/shard_map/reduce_sum | solution.py:11
  31.1 0.0 all-reduce.3.cloned.1.call-update
  31.2 0.0 all-gather.3.cloned.1.call-start
  31.2 34.4 %all-reduce.3.cloned.1.call-done = (f32[8,1024]{1,0:T(8,128)}, f32[8,1024]{1,0:T(8,128)}) async-done(((f32[8,1024]{1,0:T(8,128)}, f32[8,1024]{1,0:T(8,128)}), (f32[8,1024]{1,0:T(8,128)}, f32[8,1024]{1,0:T(8,128)})) %all-reduce.3.cloned.1.call-update) | async-done | bytes 65552 | tf_op jit(solution)/shard_map/psum | solution.py:10
  65.6 0.8 sqrt.6
  66.4 0.0 copy-start
  66.4 0.8 sqrt.7
  67.2 0.0 copy-done.3
  67.2 0.0 copy-start.1
  67.2 29.3 %divide_convert_fusion = (bf16[8,512,1024]{2,1,0:T(8,128)(2,1)}, bf16[8,512,1024]{2,1,0:T(8,128)(2,1)}) fusion(f32[8,1024]{1,0:T(8,128)S(1)} %sqrt.7, f32[8,512,1024]{2,1,0:T(8,128)} %param.10, f32[8]{0:T(128)S(1)} %broadcast_subtract_fusion, f32[8,512,1024]{2,1,0:T(8,128)} %param.9, f32[8]{0:T(128)S(1)} %copy-done.3, f32[8,1024]{1,0:T(8,128)S(1)} %sqrt.6, ...), kind=kLoop, calls=%fused_computation | loop fusion | flops 41943040 | bytes 83951680 | tf_op jit(solution)/shard_map/convert_element_type | solution.py:17
  96.6 0.0 copy-done
  96.6 0.0 copy-done.1
  96.6 0.0 copy-start.2
  96.6 0.0 copy-start.4
  96.6 0.0 all-gather.3.cloned.1.call-update
  96.6 0.0 all-gather.5.cloned.1.call-start
  96.7 0.7 all-gather.5.cloned.1.call-update
  97.4 0.0 copy-done.2
  97.4 0.0 copy-done.4
  97.4 5.2 all_gather.14
  102.6 30.9 %all_gather.15 = bf16[2048,64]{0,1:T(8,128)(2,1)S(1)} all-gather(bf16[2048,8]{0,1:T(8,128)(2,1)S(1)} %all_gather.14), channel_id=1, replica_groups=mesh['bank'=8,'zero'=4] {'bank'}, dimensions={1}, use_global_device_ids=true | all-gather | bytes 294912 | tf_op jit(solution)/shard_map/all_gather | solution.py:25
  133.5 164.8 %all-gather.3.cloned.1.call-done = bf16[8,2048,1024]{2,1,0:T(8,128)(2,1)} async-done(((bf16[8,512,1024]{2,1,0:T(8,128)(2,1)}), bf16[8,2048,1024]{2,1,0:T(8,128)(2,1)}) %all-gather.3.cloned.1.call-update) | async-done | bytes 33554448 | tf_op jit(solution)/shard_map/all_gather | solution.py:20
  298.3 203.7 %all-gather.5.cloned.1.call-done = bf16[8,2048,1024]{2,1,0:T(8,128)(2,1)} async-done(((bf16[8,512,1024]{2,1,0:T(8,128)(2,1)}), bf16[8,2048,1024]{2,1,0:T(8,128)(2,1)}) %all-gather.5.cloned.1.call-update) | async-done | bytes 33554448 | tf_op jit(solution)/shard_map/all_gather | solution.py:21
  502.0 23.2 %copy.17 = bf16[8,2048,1024]{2,1,0:T(8,128)(2,1)} copy(bf16[8,2048,1024]{2,1,0:T(8,128)(2,1)} %all-gather.3.cloned.1.call-done) | data formatting | bytes 67108864
  525.2 23.2 %copy.18 = bf16[8,2048,1024]{2,1,0:T(8,128)(2,1)} copy(bf16[8,2048,1024]{2,1,0:T(8,128)(2,1)} %all-gather.5.cloned.1.call-done) | data formatting | bytes 67108864
  548.4 0.7 copy.19
  (1 shorter events, 0.0 us)
Async XLA Ops:
  7.2 58.5 %all-reduce.3.cloned.1.call-start = ((), (), s32[]{:S(2)}) async-start(), calls=%async_computation.2 | async-start | bytes 131072 | tf_op jit(solution)/shard_map/psum | solution.py:10
  7.9 59.3 %copy-start.3 = (f32[8]{0:T(128)S(1)}, f32[8]{0:T(128)}, u32[]{:S(2)}) copy-start(f32[8]{0:T(128)} %param.11) | copy-start | bytes 100
  31.2 267.1 %all-gather.3.cloned.1.call-start = ((), (), s32[]{:S(2)}) async-start(), calls=%async_computation | async-start | bytes 41943040 | tf_op jit(solution)/shard_map/all_gather | solution.py:20
  66.4 30.2 %copy-start = (f32[8,1024]{1,0:T(8,128)}, f32[8,1024]{1,0:T(8,128)S(1)}, u32[]{:S(2)}) copy-start(f32[8,1024]{1,0:T(8,128)S(1)} %sqrt.6) | copy-start | bytes 98308
  67.2 29.4 %copy-start.1 = (f32[8,1024]{1,0:T(8,128)}, f32[8,1024]{1,0:T(8,128)S(1)}, u32[]{:S(2)}) copy-start(f32[8,1024]{1,0:T(8,128)S(1)} %sqrt.7) | copy-start | bytes 98308
  96.6 0.8 copy-start.2
  96.6 0.8 copy-start.4
  96.6 405.4 %all-gather.5.cloned.1.call-start = ((), (), s32[]{:S(2)}) async-start(), calls=%async_computation.1 | async-start | bytes 41943040 | tf_op jit(solution)/shard_map/all_gather | solution.py:21
Sparse Core Ops, SparseCore 0:
  31.3 34.3 all-reduce.2
  96.7 201.4 all-gather.2
  300.4 201.4 all-gather.4
where the time goes:
time: 556 us
  waiting for transfers between devices  404 us (73%)
  other arithmetic  53.3 us (10%)
  local copies, waits for them, and re-layouts  48.7 us (9%)
  blocking collectives  36.1 us (6%)
  between operations  13.8 us (2%)
    all_gather x1, waiting for transfers between devices, local(): lax.all_gather(narrow_up, 'zero', axis=1, tiled=True)  204 us
    all_gather x1, waiting for transfers between devices, local(): lax.all_gather(narrow_gate, 'zero', axis=1, tiled=True)  165 us
    unnamed x13, local copies, waits for them, and re-layouts  47.2 us
    psum x1, waiting for transfers between devices, local(): lax.psum((jnp.sum(fresh_gate * fresh_gate, axis=1), jnp.sum(fresh_up * fr...  34.4 us
    all_gather x1, blocking collectives, local(): serve_router = lax.all_gather(row_router, 'bank', axis=1, tiled=True)  30.9 us
    convert_element_type x1, other arithmetic, local(): (fresh_up / jnp.expand_dims(scale_up, 1)).astype(jnp.bfloat16)  29.3 us
    reduce_sum x1, other arithmetic, local(): jnp.sum(fresh_up * fresh_up, axis=1)  23.3 us
  transfers between devices with their start and end apart: 3, of which 3 were waited for; matrix products, arithmetic and copies ran while one was open for 0% of the time, Pallas kernels for 0%

commit v1 on v0

v1 whole, which is shorter than its diff:
```python
import jax
import jax.numpy as jnp
from jax import lax
from jax.experimental import pallas as pl
from jax.sharding import PartitionSpec as P


def copy_body(piece, *refs):
    refs[-1][...] = piece[...]


def place(piece, out, shape, start):
    count, rows, columns = piece.shape
    specs = [pl.BlockSpec((1, rows, columns), lambda e: (e, 0, 0))]
    operands = [piece]
    aliases = {}
    if out is not None:
        specs.append(pl.BlockSpec(memory_space=pl.ANY))
        operands.append(out)
        aliases = {1: 0}
    size = piece.size * piece.dtype.itemsize
    return pl.pallas_call(
        copy_body,
        grid=(count,),
        in_specs=specs,
        out_specs=pl.BlockSpec((1, rows, columns), lambda e: (e + start, 0, 0)),
        out_shape=jax.ShapeDtypeStruct(shape, piece.dtype),
        input_output_aliases=aliases,
        cost_estimate=pl.CostEstimate(flops=0, bytes_accessed=2 * size, transcendentals=0),
    )(*operands)


def narrow(first, second, share):
    fresh = share[:, None, None] * first + (1.0 - share[:, None, None]) * second
    parts = lax.all_gather(jnp.sum(fresh * fresh, axis=1), "zero", axis=0)
    scale = jnp.sqrt(jnp.sum(parts, axis=0))
    return scale, (fresh / jnp.expand_dims(scale, 1)).astype(jnp.bfloat16)


def local(w_gate, avg_gate, w_up, avg_up, mix_share, router_weight, router_gain):
    scale_gate, narrow_gate = narrow(w_gate, avg_gate, mix_share)
    w_up, avg_up, router_weight, narrow_gate = lax.optimization_barrier(
        (w_up, avg_up, router_weight, narrow_gate)
    )
    wide_gate = lax.all_gather(narrow_gate, "zero", axis=1, tiled=True)
    scale_up, narrow_up = narrow(w_up, avg_up, mix_share)
    experts = narrow_up.shape[0]
    last = experts // 4
    cuts = [0, experts - last, experts] if last else [0, experts]
    wide_up = []
    for a, b in zip(cuts, cuts[1:]):
        wide_up.append(lax.all_gather(narrow_up[a:b], "zero", axis=1, tiled=True))
    serve_gate = place(wide_gate, None, wide_gate.shape, 0)
    serve_up = None
    for a, piece in zip(cuts, wide_up):
        serve_up = place(piece, serve_up, wide_gate.shape, a)
    part_router = (router_weight * router_gain[:, None]).astype(jnp.bfloat16)
    row_router = lax.all_gather(part_router, "zero", axis=0, tiled=True)
    serve_router = lax.all_gather(row_router, "bank", axis=1, tiled=True)
    return (serve_gate, serve_up, scale_gate, scale_up, serve_router)


def solution(mesh):
    placed = (
        P("bank", "zero", None),
        P("bank", "zero", None),
        P("bank", "zero", None),
        P("bank", "zero", None),
        P("bank"),
        P("zero", "bank"),
        P("zero"),
    )
    return jax.shard_map(
        local,
        mesh=mesh,
        in_specs=placed,
        out_specs=(
            P("bank", None, None),
            P("bank", None, None),
            P("bank", None),
            P("bank", None),
            P(),
        ),
        check_vma=False,
    )
```

time: 556 us -> 525 us (0.944)
  waiting for transfers between devices: 404 us -> 356 us
  Pallas kernels: 0 us -> 47 us
  local copies, waits for them, and re-layouts: 48.7 us -> 10.6 us
  blocking collectives: 36.1 us -> 48.8 us
    pallas_call x0 -> x3, Pallas kernels: none -> 47 us  [place(): pl.pallas_call(copy_body, grid=(count,), in_specs=specs, out_specs=pl.Blo...]
    unnamed x13 -> x15, local copies, waits for them, and re-layouts: 47.2 us -> 4.12 us
    psum x1 -> x0, waiting for transfers between devices: 34.4 us -> none  [local(): lax.psum((jnp.sum(fresh_gate * fresh_gate, axis=1), jnp.sum(fresh_up * fr...]
    all_gather x2 -> x3, waiting for transfers between devices: 369 us -> 355 us  [the longest x1 198 us: local(): wide_gate = lax.all_gather(narrow_gate, 'zero', axis=1, tiled=True)]
    all_gather x0 -> x2, blocking collectives: none -> 12.2 us  [narrow(): parts = lax.all_gather(jnp.sum(fresh * fresh, axis=1), 'zero', axis=0)]
    convert_element_type x1 -> x2, other arithmetic: 29.3 us -> 22.8 us  [narrow(): return (scale, (fresh / jnp.expand_dims(scale, 1)).astype(jnp.bfloat16))]
    slice x0 -> x2, local copies, waits for them, and re-layouts: none -> 6.46 us  [local(): wide_up.append(lax.all_gather(narrow_up[a:b], 'zero', axis=1, tiled=True))]
    reduce_sum x1 -> x4, other arithmetic: 23.3 us -> 24.7 us  [the longest x2 24.7 us: narrow(): parts = lax.all_gather(jnp.sum(fresh * fresh, axis=1), 'zero', axis=0)]
  transfers between devices with their start and end apart: 3 -> 3, of which waited for: 3 -> 3; matrix products, arithmetic and copies ran while one was open for 0% -> 1% of each run, Pallas kernels for 0% -> 5%
where the time goes in v1:
time: 525 us; the launch traced here: 524 us
  waiting for transfers between devices  356 us (68%)
  blocking collectives  48.8 us (9%)
  other arithmetic  48.2 us (9%)
  Pallas kernels  47 us (9%)
  between operations  13.9 us (3%)
  local copies, waits for them, and re-layouts  10.6 us (2%)
    all_gather x1, waiting for transfers between devices, local(): wide_gate = lax.all_gather(narrow_gate, 'zero', axis=1, tiled=True)  198 us
    all_gather x2, waiting for transfers between devices, local(): wide_up.append(lax.all_gather(narrow_up[a:b], 'zero', axis=1, tiled=True))  157 us
    pallas_call x3, Pallas kernels, place(): pl.pallas_call(copy_body, grid=(count,), in_specs=specs, out_specs=pl.Blo...  47 us
    all_gather x1, blocking collectives, local(): serve_router = lax.all_gather(row_router, 'bank', axis=1, tiled=True)  31.4 us
    reduce_sum x2, other arithmetic, narrow(): parts = lax.all_gather(jnp.sum(fresh * fresh, axis=1), 'zero', axis=0)  24.7 us
    convert_element_type x2, other arithmetic, narrow(): return (scale, (fresh / jnp.expand_dims(scale, 1)).astype(jnp.bfloat16))  22.8 us
    all_gather x2, blocking collectives, narrow(): parts = lax.all_gather(jnp.sum(fresh * fresh, axis=1), 'zero', axis=0)  12.2 us
  transfers between devices with their start and end apart: 3, of which 3 were waited for; matrix products, arithmetic and copies ran while one was open for 1% of the time, Pallas kernels for 5%

profile of v1, /device:TPU:0, one launch (start us, length us, event | category | flops | bytes accessed | tf_op | source)
XLA Modules:
  0.0 524.3 jit_solution(12210048566954057226)
XLA Ops:
  7.2 0.0 all-gather.10.cloned.1.call-start
  7.2 0.7 broadcast_subtract_fusion
  7.9 0.0 copy-start
  7.9 0.0 copy-start.5
  7.9 12.8 %multiply_reduce_fusion.1 = f32[8,1024]{1,0:T(8,128)S(1)} fusion(f32[8,512,1024]{2,1,0:T(8,128)} %param.8, f32[8]{0:T(128)S(1)} %broadcast_subtract_fusion, f32[8,512,1024]{2,1,0:T(8,128)} %param.7, f32[8]{0:T(128)} %param.11), kind=kLoop, calls=%fused_computation.4 | loop fusion | flops 20963328 | bytes 33587264 | tf_op jit(solution)/shard_map/reduce_sum | solution.py:35
  20.6 6.6 %all-gather = f32[32,1024]{1,0:T(8,128)S(1)} all-gather(f32[8,1024]{1,0:T(8,128)S(1)} %multiply_reduce_fusion.1), channel_id=2, replica_groups=mesh['bank'=8,'zero'=4] {'zero'}, dimensions={0}, use_global_device_ids=true | all-gather | bytes 163840 | tf_op jit(solution)/shard_map/all_gather | solution.py:35
  27.3 0.0 copy-done
  27.3 0.0 copy-done.5
  27.3 0.0 copy-start.2
  27.4 10.8 %divide_convert_fusion.1 = bf16[8,512,1024]{2,1,0:T(8,128)(2,1)} fusion(f32[8,1024]{1,0:T(8,128)S(1)} %sqrt.14, f32[8,512,1024]{2,1,0:T(8,128)S(1)} %copy-done, f32[8]{0:T(128)S(1)} %broadcast_subtract_fusion, f32[8,512,1024]{2,1,0:T(8,128)} %param.7, f32[8]{0:T(128)S(1)} %copy-done.5), kind=kLoop, calls=%fused_computation.3 | loop fusion | flops 20971520 | bytes 41975872 | tf_op jit(solution)/shard_map/convert_element_type | solution.py:37
  38.1 0.0 copy-done.2
  38.1 12.0 %multiply_reduce_fusion = f32[8,1024]{1,0:T(8,128)S(1)} fusion(f32[8,512,1024]{2,1,0:T(8,128)} %param.10, f32[8]{0:T(128)S(1)} %broadcast_subtract_fusion, f32[8,512,1024]{2,1,0:T(8,128)} %param.9, f32[8]{0:T(128)S(1)} %copy-done.5), kind=kLoop, calls=%fused_computation.1 | loop fusion | flops 20963328 | bytes 33587264 | tf_op jit(solution)/shard_map/reduce_sum | solution.py:35
  50.1 5.6 %all-gather.1 = f32[32,1024]{1,0:T(8,128)S(1)} all-gather(f32[8,1024]{1,0:T(8,128)S(1)} %multiply_reduce_fusion), channel_id=3, replica_groups=mesh['bank'=8,'zero'=4] {'zero'}, dimensions={0}, use_global_device_ids=true | all-gather | bytes 163840 | tf_op jit(solution)/shard_map/all_gather | solution.py:35
  55.7 0.0 copy-start.3
  55.7 12.1 %divide_convert_fusion = bf16[8,512,1024]{2,1,0:T(8,128)(2,1)S(1)} fusion(f32[8,1024]{1,0:T(8,128)S(1)} %sqrt.15, f32[8,512,1024]{2,1,0:T(8,128)} %param.10, f32[8]{0:T(128)S(1)} %broadcast_subtract_fusion, f32[8,512,1024]{2,1,0:T(8,128)} %param.9, f32[8]{0:T(128)S(1)} %copy-done.5), kind=kLoop, calls=%fused_computation | loop fusion | flops 20971520 | bytes 41975872 | tf_op jit(solution)/shard_map/convert_element_type | solution.py:37
  67.8 0.0 copy-done.3
  67.8 0.0 copy-start.1
  67.8 3.4 copy-done.1
  71.2 0.0 copy-start.4
  71.2 0.0 copy-start.6
  71.2 3.4 slice.9
  74.6 0.0 all-gather.10.cloned.1.call-update
  74.6 0.0 all-gather.8.cloned.1.call-start
  74.7 3.1 slice.8
  77.8 0.0 all-gather.8.cloned.1.call-update
  77.8 0.0 all-gather.6.cloned.1.call-start
  77.8 0.7 all-gather.6.cloned.1.call-update
  78.5 0.0 copy-done.4
  78.5 0.0 copy-done.6
  78.6 5.2 all_gather.34
  83.8 31.4 %all_gather.35 = bf16[2048,64]{0,1:T(8,128)(2,1)S(1)} all-gather(bf16[2048,8]{0,1:T(8,128)(2,1)S(1)} %all_gather.34), channel_id=1, replica_groups=mesh['bank'=8,'zero'=4] {'bank'}, dimensions={1}, use_global_device_ids=true | all-gather | bytes 294912 | tf_op jit(solution)/shard_map/all_gather | solution.py:59
  115.2 115.9 %all-gather.10.cloned.1.call-done.piece = bf16[6,2048,1024]{2,1,0:T(8,128)(2,1)} async-done(((bf16[6,512,1024]{2,1,0:T(8,128)(2,1)}), bf16[6,2048,1024]{2,1,0:T(8,128)(2,1)}) %all-gather.10.cloned.1.call-update) | async-done | bytes 25165840 | tf_op jit(solution)/shard_map/all_gather | solution.py:52
  231.0 18.6 %shard_map.111.refs_0_ = bf16[8,2048,1024]{2,1,0:T(8,128)(2,1)} custom-call(bf16[6,2048,1024]{2,1,0:T(8,128)(2,1)} %all-gather.10.cloned.1.call-done.piece), custom_call_target="tpu_custom_call" | custom-call | bytes 50331648 | tf_op jit(solution)/shard_map/pallas_call | solution.py:22
  249.7 41.2 %all-gather.8.cloned.1.call-done.piece = bf16[2,2048,1024]{2,1,0:T(8,128)(2,1)} async-done(((bf16[2,512,1024]{2,1,0:T(8,128)(2,1)}), bf16[2,2048,1024]{2,1,0:T(8,128)(2,1)}) %all-gather.8.cloned.1.call-update) | async-done | bytes 8388624 | tf_op jit(solution)/shard_map/all_gather | solution.py:52
  290.9 5.9 %shard_map.112 = bf16[8,2048,1024]{2,1,0:T(8,128)(2,1)} custom-call(bf16[2,2048,1024]{2,1,0:T(8,128)(2,1)} %all-gather.8.cloned.1.call-done.piece, bf16[8,2048,1024]{2,1,0:T(8,128)(2,1)} %shard_map.111.refs_0_), custom_call_target="tpu_custom_call", output_to_operand_aliasing={{}: (1, {})} | custom-call | bytes 16777216 | tf_op jit(solution)/shard_map/pallas_call | solution.py:22
  296.7 197.8 %all-gather.6.cloned.1.call-done.piece = bf16[8,2048,1024]{2,1,0:T(8,128)(2,1)} async-done(((bf16[8,512,1024]{2,1,0:T(8,128)(2,1)}), bf16[8,2048,1024]{2,1,0:T(8,128)(2,1)}) %all-gather.6.cloned.1.call-update) | async-done | bytes 33554448 | tf_op jit(solution)/shard_map/all_gather | solution.py:45
  494.6 22.5 %shard_map.110 = bf16[8,2048,1024]{2,1,0:T(8,128)(2,1)} custom-call(bf16[8,2048,1024]{2,1,0:T(8,128)(2,1)} %all-gather.6.cloned.1.call-done.piece), custom_call_target="tpu_custom_call" | custom-call | bytes 67108864 | tf_op jit(solution)/shard_map/pallas_call | solution.py:22
  517.0 0.7 copy.15
  (5 shorter events, 0.1 us)
Async XLA Ops:
  7.2 223.9 %all-gather.10.cloned.1.call-start = ((), (), s32[]{:S(2)}) async-start(), calls=%async_computation.2 | async-start | bytes 31457280 | tf_op jit(solution)/shard_map/all_gather | solution.py:52
  7.9 19.5 %copy-start = (f32[8,512,1024]{2,1,0:T(8,128)S(1)}, f32[8,512,1024]{2,1,0:T(8,128)}, u32[]{:S(2)}) copy-start(f32[8,512,1024]{2,1,0:T(8,128)} %param.8) | copy-start | bytes 50331652
  7.9 19.5 %copy-start.5 = (f32[8]{0:T(128)S(1)}, f32[8]{0:T(128)}, u32[]{:S(2)}) copy-start(f32[8]{0:T(128)} %param.11) | copy-start | bytes 100
  27.3 10.8 %copy-start.2 = (f32[8,1024]{1,0:T(8,128)}, f32[8,1024]{1,0:T(8,128)S(1)}, u32[]{:S(2)}) copy-start(f32[8,1024]{1,0:T(8,128)S(1)} %sqrt.14) | copy-start | bytes 98308
  55.7 12.1 %copy-start.3 = (f32[8,1024]{1,0:T(8,128)}, f32[8,1024]{1,0:T(8,128)S(1)}, u32[]{:S(2)}) copy-start(f32[8,1024]{1,0:T(8,128)S(1)} %sqrt.15) | copy-start | bytes 98308
  67.8 3.4 copy-start.1
  71.2 7.3 %copy-start.4 = (f32[512,8]{0,1:T(8,128)S(1)}, f32[512,8]{0,1:T(8,128)}, u32[]{:S(2)}) copy-start(f32[512,8]{0,1:T(8,128)} %param.12) | copy-start | bytes 49156
  71.2 7.3 %copy-start.6 = (f32[512]{0:T(512)S(1)}, f32[512]{0:T(512)}, u32[]{:S(2)}) copy-start(f32[512]{0:T(512)} %param.13) | copy-start | bytes 6148
  74.6 216.3 %all-gather.8.cloned.1.call-start = ((), (), s32[]{:S(2)}) async-start(), calls=%async_computation.1 | async-start | bytes 10485760 | tf_op jit(solution)/shard_map/all_gather | solution.py:52
  77.8 416.8 %all-gather.6.cloned.1.call-start = ((), (), s32[]{:S(2)}) async-start(), calls=%async_computation | async-start | bytes 41943040 | tf_op jit(solution)/shard_map/all_gather | solution.py:45
Sparse Core Ops, SparseCore 0:
  74.7 156.2 all-gather.9
  232.6 58.2 all-gather.7
  293.0 201.4 all-gather.5
